TPU v7x, 32 devices: a whole 2x2x4 slice. The times are simulated.
32 devices in a mesh: dom: 8 (over y, x, core), dim: 4 (over z).
Axes of the slice: x: 2, y: 2, z: 4, core: 2. Of those that a mesh axis runs over, the one named last changes fastest.
Arguments:
- particles: float32 [64, 1024], P('dom', 'dim'), may hold values from -5 to 5
- data_rows: bfloat16 [64, 16, 1024], P('dom', None, 'dim'), may hold values from -0.375 to 0.375
- labels: int32 [64, 16], P('dom'), may hold values from 0 to 1
Outputs:
- updates: float32 [2, 64, 1024], P(None, 'dom', 'dim')
All inputs are finite; a program needn't handle non-finite values.
Results may differ from a plain program's by a relative error of at most 0.0003.
Values may be sent and summed in bfloat16 or wider, within the bound.
A program may use at most 64 MiB of HBM per device.

v0:
```python
from functools import partial
import jax
import jax.numpy as jnp
from jax import lax
from jax.sharding import PartitionSpec as P

NEWTON = 2
CG_STEPS = 2
BAND = 1
prior_precision = 0.05
like_weight = 4.0
move_size = 0.5
highest = lax.Precision.HIGHEST


def drift_terms(x_local, squares, kernel_scale, rows_pos, rows_grad):
    inner_rows = jnp.einsum("id,jd->ij", x_local, rows_pos, precision=highest)
    row_squares = jnp.sum(rows_pos * rows_pos, axis=1)
    distance = squares[:, None] + row_squares[None, :] - 2.0 * inner_rows
    kernel = jnp.exp(-distance / kernel_scale)
    kernel_sq = kernel * kernel
    kernel_grad = jnp.dot(kernel, rows_grad, precision=highest)
    kernel_pos = jnp.dot(kernel, rows_pos, precision=highest)
    square_pos = jnp.dot(kernel_sq, rows_pos, precision=highest)
    return (
        kernel,
        kernel_grad,
        kernel_pos,
        square_pos,
        jnp.sum(kernel, axis=1),
        jnp.sum(kernel_sq, axis=1),
    )


def pair_block(running, piece, start, kernel, curve_rows, pos_rows, vectors, cross_scale):
    weight_sq = (kernel * kernel).T
    factor_part = piece.astype(jnp.float32)
    projected = jnp.einsum("jrd,id->jri", factor_part, vectors, precision=highest)
    weighted = projected * curve_rows[:, :, None] * weight_sq[:, None, :]
    running = jnp.einsum("jrd,jri->id", factor_part, weighted, precision=highest)
    along_pair = jnp.einsum("jd,id->ji", pos_rows, vectors, precision=highest)
    return running + cross_scale * jnp.einsum(
        "ji,jd->id", weight_sq * along_pair, pos_rows, precision=highest
    )


def residual_sum(vectors):
    return lax.psum(jnp.sum(vectors * vectors), ("dom", "dim"))


def per_device(particles, data_rows, labels):
    dim_count = lax.axis_size("dim")
    dom_count = lax.axis_size("dom")
    part_rows = particles.shape[0]
    slice_width = particles.shape[1]
    width = slice_width * dim_count
    quarter = part_rows // dim_count
    total_count = part_rows * dom_count
    kernel_scale = 1.0 * BAND * width
    cross_scale = 4.0 / (kernel_scale * kernel_scale)
    lane = lax.axis_index("dim")
    first_row = lane * quarter
    first_col = lane * slice_width
    own_factors = lax.all_to_all(data_rows, "dim", split_axis=0, concat_axis=2, tiled=True)
    factor_float = own_factors.astype(jnp.float32)
    own_targets = lax.dynamic_slice_in_dim(labels, first_row, quarter, 0).astype(jnp.float32)
    current = particles
    outputs = []
    for newton_step in range(NEWTON):
        x_local = lax.all_gather(current, "dim", axis=1, tiled=True)
        own_pos = lax.dynamic_slice_in_dim(x_local, first_row, quarter, 0)
        logits = jnp.einsum("jrd,jd->jr", factor_float, own_pos, precision=highest)
        probs = jax.nn.sigmoid(logits)
        own_grad = -prior_precision * own_pos + like_weight * jnp.einsum(
            "jr,jrd->jd", own_targets - probs, factor_float, precision=highest
        )
        own_curve = like_weight * probs * (1.0 - probs)
        pos_rows, grad_rows, curve_rows = (
            lax.all_gather(own_pos, "dom", axis=0, tiled=True),
            lax.all_gather(own_grad, "dom", axis=0, tiled=True),
            lax.all_gather(own_curve, "dom", axis=0, tiled=True),
        )
        squares = jnp.sum(x_local * x_local, axis=1)
        kernel, kernel_grad, kernel_pos, square_pos, kernel_total, square_total = drift_terms(
            x_local, squares, kernel_scale, pos_rows, grad_rows
        )
        kernel_grad, kernel_pos, square_pos, kernel_total, square_total = lax.psum(
            (kernel_grad, kernel_pos, square_pos, kernel_total, square_total), "dim"
        )
        drift_full = (
            kernel_grad + 2.0 / kernel_scale * (x_local * kernel_total[:, None] - kernel_pos)
        ) / total_count
        drift = lax.dynamic_slice_in_dim(drift_full, first_col, slice_width, 1)
        mean_slice = lax.dynamic_slice_in_dim(square_pos, first_col, slice_width, 1)
        solution = jnp.zeros_like(drift)
        residual = drift
        direction = drift
        norm_now = residual_sum(residual)
        for solve_step in range(CG_STEPS):
            vectors_full = lax.all_gather(direction, "dim", axis=1, tiled=True)
            start_total = jnp.zeros((part_rows, width), jnp.float32)
            block_step = partial(
                pair_block,
                kernel=kernel,
                curve_rows=curve_rows,
                pos_rows=pos_rows,
                vectors=vectors_full,
                cross_scale=cross_scale,
            )
            pairs = block_step(
                start_total, lax.all_gather(own_factors, "dom", axis=0, tiled=True), jnp.int32(0)
            )
            pairs = lax.psum_scatter(pairs, "dim", scatter_dimension=1, tiled=True)
            along_self = jnp.sum(x_local * vectors_full, axis=1)
            along_mean = jnp.sum(vectors_full * square_pos, axis=1)
            local = prior_precision * square_total[:, None] * direction + cross_scale * (
                current * (along_self * square_total - along_mean)[:, None]
                - along_self[:, None] * mean_slice
            )
            image = (pairs + local) / total_count
            curve_total, mixed_total, image_square = lax.psum(
                (jnp.sum(direction * image), jnp.sum(residual * image), jnp.sum(image * image)),
                ("dom", "dim"),
            )
            alpha = norm_now / curve_total
            norm_next = norm_now - 2.0 * alpha * mixed_total + alpha * alpha * image_square
            solution = solution + alpha * direction
            residual = residual - alpha * image
            if solve_step + 1 < CG_STEPS:
                direction = residual + norm_next / norm_now * direction
                norm_now = norm_next
        outputs.append(solution)
        current = current + move_size * solution
    return jnp.stack(outputs)


def solution(mesh):
    placed = (P("dom", "dim"), P("dom", None, "dim"), P("dom", None))
    return jax.shard_map(
        per_device, mesh=mesh, in_specs=placed, out_specs=P(None, "dom", "dim"), check_vma=False
    )
```

profile of v0, /device:TPU:12, one launch (start us, length us, event | category | flops | bytes accessed | tf_op | source)
XLA Modules:
  0.0 489.8 jit_solution(9462814069500571010)
XLA Ops:
  6.5 5.3 %all-to-all-start = ((bf16[8,16,256]{2,1,0:T(8,128)(2,1)}), bf16[8,16,256]{2,1,0:T(8,128)(2,1)S(1)}, u32[]{:S(2)}, u32[]{:S(2)}) async-start(bf16[8,16,256]{2,1,0:T(8,128)(2,1)} %param.4), calls=%async_computation | async-start | bytes 131072 | tf_op jit(solution)/shard_map/all_to_all | solution.py:64
  12.6 13.1 %all_gather.42 = f32[8,1024]{1,0:T(8,128)S(1)} all-gather(f32[8,256]{1,0:T(8,128)S(1)} %copy-done.2), channel_id=1, replica_groups=mesh['dom'=8,'dim'=4] {'dim'}, dimensions={1}, use_global_device_ids=true | all-gather | bytes 40960 | tf_op jit(solution)/shard_map/all_gather | solution.py:70
  27.0 9.2 %all-gather = f32[8,2,1024]{2,1,0:T(2,128)S(1)} all-gather(f32[1,2,1024]{2,1,0:T(2,128)S(1)} %get-tuple-element.47), channel_id=1, replica_groups=mesh['dom'=8,'dim'=4] {'dom'}, dimensions={0}, use_global_device_ids=true | all-gather | bytes 73728 | tf_op jit(solution)/shard_map/all_gather | solution.py:79
  39.0 8.3 %all-gather.1 = f32[8,2,1024]{2,1,0:T(2,128)S(1)} all-gather(f32[1,2,1024]{2,1,0:T(2,128)S(1)} %get-tuple-element.48), channel_id=1, replica_groups=mesh['dom'=8,'dim'=4] {'dom'}, dimensions={0}, use_global_device_ids=true | all-gather | bytes 73728 | tf_op jit(solution)/shard_map/all_gather | solution.py:80
  48.2 8.9 %all-gather.2 = f32[8,2,16]{2,1,0:T(2,128)S(1)} all-gather(f32[1,2,16]{2,1,0:T(2,128)S(1)} %get-tuple-element.43), channel_id=1, replica_groups=mesh['dom'=8,'dim'=4] {'dom'}, dimensions={0}, use_global_device_ids=true | all-gather | bytes 1152 | tf_op jit(solution)/shard_map/all_gather | solution.py:81
  57.2 8.9 %all_gather.46 = bf16[16,16,1024]{2,1,0:T(8,128)(2,1)S(1)} all-gather(bf16[2,16,1024]{2,1,0:T(8,128)(2,1)S(1)} %all_to_all.16), channel_id=1, replica_groups=mesh['dom'=8,'dim'=4] {'dom'}, dimensions={0}, use_global_device_ids=true | all-gather | bytes 589824 | tf_op jit(solution)/shard_map/all_gather | solution.py:111
  66.1 26.1 %all-reduce.9.cloned.1.call-done = (f32[8,1024]{1,0:T(8,128)}, f32[8,1024]{1,0:T(8,128)}, f32[8]{0:T(128)}, f32[8,1024]{1,0:T(8,128)}, f32[8]{0:T(128)}) async-done(((f32[8,1024]{1,0:T(8,128)}, f32[8,1024]{1,0:T(8,128)}, f32[8]{0:T(128)}, f32[8,1024]{1,0:T(8,128)}, f32[8]{0:T(128)}), (f32[8,1024]{1,0:T(8,128)}, f32[8,1024]{1,0:T(8,128)}, f32[8]{0:T(128)}, f32[8,1024]{1,0:T(8,128)}, ...) | async-done | bytes 98384 | tf_op jit(solution)/shard_map/psum | solution.py:87
  93.6 12.2 %all_gather.45 = f32[8,1024]{1,0:T(8,128)S(1)} all-gather(f32[8,256]{1,0:T(8,128)S(1)} %fusion.18), channel_id=1, replica_groups=mesh['dom'=8,'dim'=4] {'dim'}, dimensions={1}, use_global_device_ids=true | all-gather | bytes 40960 | tf_op jit(solution)/shard_map/all_gather | solution.py:100
  110.8 16.8 %reduce-scatter.5.cloned.1.call-done = f32[8,256]{1,0:T(8,128)} async-done(((f32[8,1024]{1,0:T(8,128)}), f32[8,256]{1,0:T(8,128)}) %reduce-scatter.5.cloned.1.call-update) | async-done | bytes 8208 | tf_op jit(solution)/shard_map/reduce_scatter | solution.py:113
  129.1 43.2 %all-reduce.1 = (f32[]{:T(128)}, f32[]{:T(128)}, f32[]{:T(128)}) all-reduce(f32[]{:T(128)} %get-tuple-element.18, f32[]{:T(128)} %get-tuple-element.17, f32[]{:T(128)} %get-tuple-element.16), channel_id=1, replica_groups=mesh['dom'=8,'dim'=4] {'dom','dim'}, use_global_device_ids=true, to_apply=%region_7.0 | all-reduce | flops 3 | bytes 24 | tf_op jit(solution)/shard_map/psum | solution.py:48
  176.2 11.4 %all_gather.48 = f32[8,1024]{1,0:T(8,128)S(1)} all-gather(f32[8,256]{1,0:T(8,128)S(1)} %multiply_add_fusion.3), channel_id=1, replica_groups=mesh['dom'=8,'dim'=4] {'dim'}, dimensions={1}, use_global_device_ids=true | all-gather | bytes 40960 | tf_op jit(solution)/shard_map/all_gather | solution.py:100
  191.4 16.5 %reduce-scatter.7.cloned.1.call-done = f32[8,256]{1,0:T(8,128)} async-done(((f32[8,1024]{1,0:T(8,128)}), f32[8,256]{1,0:T(8,128)}) %reduce-scatter.7.cloned.1.call-update) | async-done | bytes 8208 | tf_op jit(solution)/shard_map/reduce_scatter | solution.py:113
  209.4 43.1 %psum.140 = f32[]{:T(128)} all-reduce(f32[]{:T(128)} %multiply_reduce_fusion.16), channel_id=1, replica_groups=mesh['dom'=8,'dim'=4] {'dom','dim'}, use_global_device_ids=true, to_apply=%region_22.0 | all-reduce | flops 1 | bytes 8 | tf_op jit(solution)/shard_map/psum | solution.py:121
  253.2 11.3 %all_gather.49 = f32[8,1024]{1,0:T(8,128)S(1)} all-gather(f32[8,256]{1,0:T(8,128)S(1)} %get-tuple-element.50), channel_id=1, replica_groups=mesh['dom'=8,'dim'=4] {'dim'}, dimensions={1}, use_global_device_ids=true | all-gather | bytes 40960 | tf_op jit(solution)/shard_map/all_gather | solution.py:70
  265.0 8.3 %all-gather.3 = f32[8,2,1024]{2,1,0:T(2,128)S(1)} all-gather(f32[1,2,1024]{2,1,0:T(2,128)S(1)} %get-tuple-element.45), channel_id=1, replica_groups=mesh['dom'=8,'dim'=4] {'dom'}, dimensions={0}, use_global_device_ids=true | all-gather | bytes 73728 | tf_op jit(solution)/shard_map/all_gather | solution.py:79
  276.0 9.2 %all-gather.4 = f32[8,2,1024]{2,1,0:T(2,128)S(1)} all-gather(f32[1,2,1024]{2,1,0:T(2,128)S(1)} %get-tuple-element.46), channel_id=1, replica_groups=mesh['dom'=8,'dim'=4] {'dom'}, dimensions={0}, use_global_device_ids=true | all-gather | bytes 73728 | tf_op jit(solution)/shard_map/all_gather | solution.py:80
  286.3 8.0 %all-gather.5 = f32[8,2,16]{2,1,0:T(2,128)S(1)} all-gather(f32[1,2,16]{2,1,0:T(2,128)S(1)} %get-tuple-element.40), channel_id=1, replica_groups=mesh['dom'=8,'dim'=4] {'dom'}, dimensions={0}, use_global_device_ids=true | all-gather | bytes 1152 | tf_op jit(solution)/shard_map/all_gather | solution.py:81
  294.3 26.9 %all-reduce.7.cloned.1.call-done = (f32[8,1024]{1,0:T(8,128)}, f32[8,1024]{1,0:T(8,128)}, f32[8]{0:T(128)}, f32[8,1024]{1,0:T(8,128)}, f32[8]{0:T(128)}) async-done(((f32[8,1024]{1,0:T(8,128)}, f32[8,1024]{1,0:T(8,128)}, f32[8]{0:T(128)}, f32[8,1024]{1,0:T(8,128)}, f32[8]{0:T(128)}), (f32[8,1024]{1,0:T(8,128)}, f32[8,1024]{1,0:T(8,128)}, f32[8]{0:T(128)}, f32[8,1024]{1,0:T(8,128)}, ...) | async-done | bytes 98384 | tf_op jit(solution)/shard_map/psum | solution.py:87
  322.6 12.4 %all_gather.52 = f32[8,1024]{1,0:T(8,128)S(1)} all-gather(f32[8,256]{1,0:T(8,128)S(1)} %fusion.16), channel_id=1, replica_groups=mesh['dom'=8,'dim'=4] {'dim'}, dimensions={1}, use_global_device_ids=true | all-gather | bytes 40960 | tf_op jit(solution)/shard_map/all_gather | solution.py:100
  340.1 16.8 %reduce-scatter.9.cloned.1.call-done = f32[8,256]{1,0:T(8,128)} async-done(((f32[8,1024]{1,0:T(8,128)}), f32[8,256]{1,0:T(8,128)}) %reduce-scatter.9.cloned.1.call-update) | async-done | bytes 8208 | tf_op jit(solution)/shard_map/reduce_scatter | solution.py:113
  358.3 43.2 %all-reduce = (f32[]{:T(128)}, f32[]{:T(128)}, f32[]{:T(128)}) all-reduce(f32[]{:T(128)} %get-tuple-element.15, f32[]{:T(128)} %get-tuple-element.14, f32[]{:T(128)} %get-tuple-element.13), channel_id=1, replica_groups=mesh['dom'=8,'dim'=4] {'dom','dim'}, use_global_device_ids=true, to_apply=%region_30.0 | all-reduce | flops 3 | bytes 24 | tf_op jit(solution)/shard_map/psum | solution.py:48
  405.4 11.4 %all_gather.54 = f32[8,1024]{1,0:T(8,128)S(1)} all-gather(f32[8,256]{1,0:T(8,128)S(1)} %multiply_add_fusion), channel_id=1, replica_groups=mesh['dom'=8,'dim'=4] {'dim'}, dimensions={1}, use_global_device_ids=true | all-gather | bytes 40960 | tf_op jit(solution)/shard_map/all_gather | solution.py:100
  420.6 16.6 %reduce-scatter.11.cloned.1.call-done = f32[8,256]{1,0:T(8,128)} async-done(((f32[8,1024]{1,0:T(8,128)}), f32[8,256]{1,0:T(8,128)}) %reduce-scatter.11.cloned.1.call-update) | async-done | bytes 8208 | tf_op jit(solution)/shard_map/reduce_scatter | solution.py:113
  438.6 43.1 %psum.149 = f32[]{:T(128)} all-reduce(f32[]{:T(128)} %multiply_reduce_fusion.12), channel_id=1, replica_groups=mesh['dom'=8,'dim'=4] {'dom','dim'}, use_global_device_ids=true, to_apply=%region_45.0 | all-reduce | flops 1 | bytes 8 | tf_op jit(solution)/shard_map/psum | solution.py:121
  (98 shorter events, 36.8 us)
Async XLA Ops:
  6.5 19.3 %all-to-all-start = ((bf16[8,16,256]{2,1,0:T(8,128)(2,1)}), bf16[8,16,256]{2,1,0:T(8,128)(2,1)S(1)}, u32[]{:S(2)}, u32[]{:S(2)}) async-start(bf16[8,16,256]{2,1,0:T(8,128)(2,1)} %param.4), calls=%async_computation | async-start | bytes 131072 | tf_op jit(solution)/shard_map/all_to_all | solution.py:64
  11.9 0.7 copy-start.2
  11.9 80.3 %all-reduce.9.cloned.1.call-start = ((), (), s32[]{:S(2)}) async-start(), calls=%async_computation.10 | async-start | bytes 198656 | tf_op jit(solution)/shard_map/psum | solution.py:87
  26.1 0.7 copy-start.5
  57.1 70.5 %reduce-scatter.5.cloned.1.call-start = ((), (), s32[]{:S(2)}) async-start(), calls=%async_computation.5 | async-start | bytes 40960 | tf_op jit(solution)/shard_map/reduce_scatter | solution.py:113
  92.1 0.6 copy-start.7
  105.8 0.8 copy-start.1
  110.1 97.9 %reduce-scatter.7.cloned.1.call-start = ((), (), s32[]{:S(2)}) async-start(), calls=%async_computation.6 | async-start | bytes 40960 | tf_op jit(solution)/shard_map/reduce_scatter | solution.py:113
  110.2 0.7 copy-start.4
  191.4 129.8 %all-reduce.7.cloned.1.call-start = ((), (), s32[]{:S(2)}) async-start(), calls=%async_computation.9 | async-start | bytes 198656 | tf_op jit(solution)/shard_map/psum | solution.py:87
  286.1 70.7 %reduce-scatter.9.cloned.1.call-start = ((), (), s32[]{:S(2)}) async-start(), calls=%async_computation.7 | async-start | bytes 40960 | tf_op jit(solution)/shard_map/reduce_scatter | solution.py:113
  321.2 0.6 copy-start.6
  335.0 0.8 copy-start
  339.3 97.9 %reduce-scatter.11.cloned.1.call-start = ((), (), s32[]{:S(2)}) async-start(), calls=%async_computation.8 | async-start | bytes 40960 | tf_op jit(solution)/shard_map/reduce_scatter | solution.py:113
  339.4 0.7 copy-start.3
Sparse Core Ops, SparseCore 0:
  57.3 34.8 all-reduce.8
  110.2 17.3 reduce-scatter.4
  191.5 16.4 reduce-scatter.6
  286.3 34.8 all-reduce.6
  339.4 17.3 reduce-scatter.8
  420.7 16.4 reduce-scatter.10
where the time goes:
time: 492 us; the launch traced here: 490 us
  blocking collectives  305 us (62%)
  waiting for transfers between devices  120 us (24%)
  between operations  22.8 us (5%)
  matrix products  21.7 us (4%)
  other arithmetic  9.23 us (2%)
  local copies, waits for them, and re-layouts  5.56 us (1%)
  starting transfers between devices  5.53 us (1%)
    psum x2, blocking collectives, residual_sum(): return lax.psum(jnp.sum(vectors * vectors), ('dom', 'dim'))  86.5 us
    psum x2, blocking collectives, per_device(): lax.psum((jnp.sum(direction * image), jnp.sum(residual * image), jnp.sum(...  86.1 us
    reduce_scatter x4, waiting for transfers between devices, per_device(): pairs = lax.psum_scatter(pairs, 'dim', scatter_dimension=1, tiled=True)  66.7 us
    psum x2, waiting for transfers between devices, per_device(): lax.psum((kernel_grad, kernel_pos, square_pos, kernel_total, square_total...  53 us
    all_gather x4, blocking collectives, per_device(): vectors_full = lax.all_gather(direction, 'dim', axis=1, tiled=True)  47.4 us
    all_gather x2, blocking collectives, per_device(): x_local = lax.all_gather(current, 'dim', axis=1, tiled=True)  24.5 us
    all_gather x2, blocking collectives, per_device(): lax.all_gather(own_pos, 'dom', axis=0, tiled=True)  17.5 us
    all_gather x2, blocking collectives, per_device(): lax.all_gather(own_grad, 'dom', axis=0, tiled=True)  17.5 us
  transfers between devices with their start and end apart: 7, of which 6 were waited for; matrix products, arithmetic and copies ran while one was open for 0% of the time, Pallas kernels for 0%

commit v1 on v0

--- a/solution.py
+++ b/solution.py
@@ -97,7 +97,7 @@
         direction = drift
         norm_now = residual_sum(residual)
         for solve_step in range(CG_STEPS):
-            vectors_full = lax.all_gather(direction, "dim", axis=1, tiled=True)
+            vectors_full = jnp.concatenate(lax.all_gather(direction, "dim"), axis=1)
             start_total = jnp.zeros((part_rows, width), jnp.float32)
             block_step = partial(
                 pair_block,

time: 492 us -> 492 us (level)
  no operation moved by 1% of the time
where the time goes in v1:
time: 492 us; the launch traced here: 490 us
  blocking collectives  305 us (62%)
  waiting for transfers between devices  120 us (24%)
  between operations  22.8 us (5%)
  matrix products  21.7 us (4%)
  other arithmetic  9.23 us (2%)
  local copies, waits for them, and re-layouts  5.56 us (1%)
  starting transfers between devices  5.53 us (1%)
    psum x2, blocking collectives, residual_sum(): return lax.psum(jnp.sum(vectors * vectors), ('dom', 'dim'))  86.4 us
    psum x2, blocking collectives, per_device(): lax.psum((jnp.sum(direction * image), jnp.sum(residual * image), jnp.sum(...  86.1 us
    reduce_scatter x4, waiting for transfers between devices, per_device(): pairs = lax.psum_scatter(pairs, 'dim', scatter_dimension=1, tiled=True)  66.7 us
    psum x2, waiting for transfers between devices, per_device(): lax.psum((kernel_grad, kernel_pos, square_pos, kernel_total, square_total...  53 us
    all_gather x4, blocking collectives, per_device(): vectors_full = jnp.concatenate(lax.all_gather(direction, 'dim'), axis=1)  47.4 us
    all_gather x2, blocking collectives, per_device(): x_local = lax.all_gather(current, 'dim', axis=1, tiled=True)  24.5 us
    all_gather x2, blocking collectives, per_device(): lax.all_gather(own_pos, 'dom', axis=0, tiled=True)  17.5 us
    all_gather x2, blocking collectives, per_device(): lax.all_gather(own_grad, 'dom', axis=0, tiled=True)  17.5 us
  transfers between devices with their start and end apart: 7, of which 6 were waited for; matrix products, arithmetic and copies ran while one was open for 0% of the time, Pallas kernels for 0%

profile of v1, /device:TPU:12, one launch (start us, length us, event | category | flops | bytes accessed | tf_op | source)
XLA Modules:
  0.0 489.7 jit_solution(14536476329216031477)
XLA Ops:
  6.5 5.3 %all-to-all-start = ((bf16[8,16,256]{2,1,0:T(8,128)(2,1)}), bf16[8,16,256]{2,1,0:T(8,128)(2,1)S(1)}, u32[]{:S(2)}, u32[]{:S(2)}) async-start(bf16[8,16,256]{2,1,0:T(8,128)(2,1)} %param.4), calls=%async_computation | async-start | bytes 131072 | tf_op jit(solution)/shard_map/all_to_all | solution.py:64
  12.6 13.1 %all_gather.54 = f32[8,1024]{1,0:T(8,128)S(1)} all-gather(f32[8,256]{1,0:T(8,128)S(1)} %copy-done.2), channel_id=1, replica_groups=mesh['dom'=8,'dim'=4] {'dim'}, dimensions={1}, use_global_device_ids=true | all-gather | bytes 40960 | tf_op jit(solution)/shard_map/all_gather | solution.py:70
  27.0 9.2 %all-gather.4 = f32[8,2,1024]{2,1,0:T(2,128)S(1)} all-gather(f32[1,2,1024]{2,1,0:T(2,128)S(1)} %get-tuple-element.47), channel_id=1, replica_groups=mesh['dom'=8,'dim'=4] {'dom'}, dimensions={0}, use_global_device_ids=true | all-gather | bytes 73728 | tf_op jit(solution)/shard_map/all_gather | solution.py:79
  39.0 8.3 %all-gather.5 = f32[8,2,1024]{2,1,0:T(2,128)S(1)} all-gather(f32[1,2,1024]{2,1,0:T(2,128)S(1)} %get-tuple-element.48), channel_id=1, replica_groups=mesh['dom'=8,'dim'=4] {'dom'}, dimensions={0}, use_global_device_ids=true | all-gather | bytes 73728 | tf_op jit(solution)/shard_map/all_gather | solution.py:80
  48.2 8.9 %all-gather.6 = f32[8,2,16]{2,1,0:T(2,128)S(1)} all-gather(f32[1,2,16]{2,1,0:T(2,128)S(1)} %get-tuple-element.43), channel_id=1, replica_groups=mesh['dom'=8,'dim'=4] {'dom'}, dimensions={0}, use_global_device_ids=true | all-gather | bytes 1152 | tf_op jit(solution)/shard_map/all_gather | solution.py:81
  57.2 8.9 %all_gather.59 = bf16[16,16,1024]{2,1,0:T(8,128)(2,1)S(1)} all-gather(bf16[2,16,1024]{2,1,0:T(8,128)(2,1)S(1)} %all_to_all.16), channel_id=1, replica_groups=mesh['dom'=8,'dim'=4] {'dom'}, dimensions={0}, use_global_device_ids=true | all-gather | bytes 589824 | tf_op jit(solution)/shard_map/all_gather | solution.py:111
  66.1 26.1 %all-reduce.9.cloned.1.call-done = (f32[8,1024]{1,0:T(8,128)}, f32[8,1024]{1,0:T(8,128)}, f32[8]{0:T(128)}, f32[8,1024]{1,0:T(8,128)}, f32[8]{0:T(128)}) async-done(((f32[8,1024]{1,0:T(8,128)}, f32[8,1024]{1,0:T(8,128)}, f32[8]{0:T(128)}, f32[8,1024]{1,0:T(8,128)}, f32[8]{0:T(128)}), (f32[8,1024]{1,0:T(8,128)}, f32[8,1024]{1,0:T(8,128)}, f32[8]{0:T(128)}, f32[8,1024]{1,0:T(8,128)}, ...) | async-done | bytes 98384 | tf_op jit(solution)/shard_map/psum | solution.py:87
  93.6 12.2 %all-gather = f32[32,256]{1,0:T(8,128)S(1)} all-gather(f32[8,256]{1,0:T(8,128)S(1)} %fusion.14), channel_id=2, replica_groups=mesh['dom'=8,'dim'=4] {'dim'}, dimensions={0}, use_global_device_ids=true | all-gather | bytes 40960 | tf_op jit(solution)/shard_map/all_gather | solution.py:100
  110.8 16.8 %reduce-scatter.5.cloned.1.call-done = f32[8,256]{1,0:T(8,128)} async-done(((f32[8,1024]{1,0:T(8,128)}), f32[8,256]{1,0:T(8,128)}) %reduce-scatter.5.cloned.1.call-update) | async-done | bytes 8208 | tf_op jit(solution)/shard_map/reduce_scatter | solution.py:113
  129.1 43.2 %all-reduce.1 = (f32[]{:T(128)}, f32[]{:T(128)}, f32[]{:T(128)}) all-reduce(f32[]{:T(128)} %get-tuple-element.18, f32[]{:T(128)} %get-tuple-element.17, f32[]{:T(128)} %get-tuple-element.16), channel_id=1, replica_groups=mesh['dom'=8,'dim'=4] {'dom','dim'}, use_global_device_ids=true, to_apply=%region_7.0 | all-reduce | flops 3 | bytes 24 | tf_op jit(solution)/shard_map/psum | solution.py:48
  176.2 11.4 %all-gather.1 = f32[32,256]{1,0:T(8,128)S(1)} all-gather(f32[8,256]{1,0:T(8,128)S(1)} %multiply_add_fusion.3), channel_id=3, replica_groups=mesh['dom'=8,'dim'=4] {'dim'}, dimensions={0}, use_global_device_ids=true | all-gather | bytes 40960 | tf_op jit(solution)/shard_map/all_gather | solution.py:100
  191.4 16.5 %reduce-scatter.7.cloned.1.call-done = f32[8,256]{1,0:T(8,128)} async-done(((f32[8,1024]{1,0:T(8,128)}), f32[8,256]{1,0:T(8,128)}) %reduce-scatter.7.cloned.1.call-update) | async-done | bytes 8208 | tf_op jit(solution)/shard_map/reduce_scatter | solution.py:113
  209.3 43.1 %psum.140 = f32[]{:T(128)} all-reduce(f32[]{:T(128)} %multiply_reduce_fusion.16), channel_id=1, replica_groups=mesh['dom'=8,'dim'=4] {'dom','dim'}, use_global_device_ids=true, to_apply=%region_22.0 | all-reduce | flops 1 | bytes 8 | tf_op jit(solution)/shard_map/psum | solution.py:121
  253.1 11.4 %all_gather.63 = f32[8,1024]{1,0:T(8,128)S(1)} all-gather(f32[8,256]{1,0:T(8,128)S(1)} %get-tuple-element.50), channel_id=1, replica_groups=mesh['dom'=8,'dim'=4] {'dim'}, dimensions={1}, use_global_device_ids=true | all-gather | bytes 40960 | tf_op jit(solution)/shard_map/all_gather | solution.py:70
  265.0 8.3 %all-gather.7 = f32[8,2,1024]{2,1,0:T(2,128)S(1)} all-gather(f32[1,2,1024]{2,1,0:T(2,128)S(1)} %get-tuple-element.45), channel_id=1, replica_groups=mesh['dom'=8,'dim'=4] {'dom'}, dimensions={0}, use_global_device_ids=true | all-gather | bytes 73728 | tf_op jit(solution)/shard_map/all_gather | solution.py:79
  276.0 9.2 %all-gather.8 = f32[8,2,1024]{2,1,0:T(2,128)S(1)} all-gather(f32[1,2,1024]{2,1,0:T(2,128)S(1)} %get-tuple-element.46), channel_id=1, replica_groups=mesh['dom'=8,'dim'=4] {'dom'}, dimensions={0}, use_global_device_ids=true | all-gather | bytes 73728 | tf_op jit(solution)/shard_map/all_gather | solution.py:80
  286.3 8.0 %all-gather.9 = f32[8,2,16]{2,1,0:T(2,128)S(1)} all-gather(f32[1,2,16]{2,1,0:T(2,128)S(1)} %get-tuple-element.40), channel_id=1, replica_groups=mesh['dom'=8,'dim'=4] {'dom'}, dimensions={0}, use_global_device_ids=true | all-gather | bytes 1152 | tf_op jit(solution)/shard_map/all_gather | solution.py:81
  294.3 26.9 %all-reduce.7.cloned.1.call-done = (f32[8,1024]{1,0:T(8,128)}, f32[8,1024]{1,0:T(8,128)}, f32[8]{0:T(128)}, f32[8,1024]{1,0:T(8,128)}, f32[8]{0:T(128)}) async-done(((f32[8,1024]{1,0:T(8,128)}, f32[8,1024]{1,0:T(8,128)}, f32[8]{0:T(128)}, f32[8,1024]{1,0:T(8,128)}, f32[8]{0:T(128)}), (f32[8,1024]{1,0:T(8,128)}, f32[8,1024]{1,0:T(8,128)}, f32[8]{0:T(128)}, f32[8,1024]{1,0:T(8,128)}, ...) | async-done | bytes 98384 | tf_op jit(solution)/shard_map/psum | solution.py:87
  322.6 12.4 %all-gather.2 = f32[32,256]{1,0:T(8,128)S(1)} all-gather(f32[8,256]{1,0:T(8,128)S(1)} %fusion.12), channel_id=4, replica_groups=mesh['dom'=8,'dim'=4] {'dim'}, dimensions={0}, use_global_device_ids=true | all-gather | bytes 40960 | tf_op jit(solution)/shard_map/all_gather | solution.py:100
  340.0 16.8 %reduce-scatter.9.cloned.1.call-done = f32[8,256]{1,0:T(8,128)} async-done(((f32[8,1024]{1,0:T(8,128)}), f32[8,256]{1,0:T(8,128)}) %reduce-scatter.9.cloned.1.call-update) | async-done | bytes 8208 | tf_op jit(solution)/shard_map/reduce_scatter | solution.py:113
  358.3 43.2 %all-reduce = (f32[]{:T(128)}, f32[]{:T(128)}, f32[]{:T(128)}) all-reduce(f32[]{:T(128)} %get-tuple-element.15, f32[]{:T(128)} %get-tuple-element.14, f32[]{:T(128)} %get-tuple-element.13), channel_id=1, replica_groups=mesh['dom'=8,'dim'=4] {'dom','dim'}, use_global_device_ids=true, to_apply=%region_30.0 | all-reduce | flops 3 | bytes 24 | tf_op jit(solution)/shard_map/psum | solution.py:48
  405.4 11.4 %all-gather.3 = f32[32,256]{1,0:T(8,128)S(1)} all-gather(f32[8,256]{1,0:T(8,128)S(1)} %multiply_add_fusion), channel_id=5, replica_groups=mesh['dom'=8,'dim'=4] {'dim'}, dimensions={0}, use_global_device_ids=true | all-gather | bytes 40960 | tf_op jit(solution)/shard_map/all_gather | solution.py:100
  420.6 16.6 %reduce-scatter.11.cloned.1.call-done = f32[8,256]{1,0:T(8,128)} async-done(((f32[8,1024]{1,0:T(8,128)}), f32[8,256]{1,0:T(8,128)}) %reduce-scatter.11.cloned.1.call-update) | async-done | bytes 8208 | tf_op jit(solution)/shard_map/reduce_scatter | solution.py:113
  438.5 43.1 %psum.149 = f32[]{:T(128)} all-reduce(f32[]{:T(128)} %multiply_reduce_fusion.12), channel_id=1, replica_groups=mesh['dom'=8,'dim'=4] {'dom','dim'}, use_global_device_ids=true, to_apply=%region_45.0 | all-reduce | flops 1 | bytes 8 | tf_op jit(solution)/shard_map/psum | solution.py:121
  (98 shorter events, 36.8 us)
Async XLA Ops:
  6.5 19.3 %all-to-all-start = ((bf16[8,16,256]{2,1,0:T(8,128)(2,1)}), bf16[8,16,256]{2,1,0:T(8,128)(2,1)S(1)}, u32[]{:S(2)}, u32[]{:S(2)}) async-start(bf16[8,16,256]{2,1,0:T(8,128)(2,1)} %param.4), calls=%async_computation | async-start | bytes 131072 | tf_op jit(solution)/shard_map/all_to_all | solution.py:64
  11.9 0.7 copy-start.2
  11.9 80.3 %all-reduce.9.cloned.1.call-start = ((), (), s32[]{:S(2)}) async-start(), calls=%async_computation.10 | async-start | bytes 198656 | tf_op jit(solution)/shard_map/psum | solution.py:87
  26.1 0.7 copy-start.5
  57.1 70.5 %reduce-scatter.5.cloned.1.call-start = ((), (), s32[]{:S(2)}) async-start(), calls=%async_computation.5 | async-start | bytes 40960 | tf_op jit(solution)/shard_map/reduce_scatter | solution.py:113
  92.1 0.6 copy-start.7
  105.8 0.8 copy-start.1
  110.1 97.9 %reduce-scatter.7.cloned.1.call-start = ((), (), s32[]{:S(2)}) async-start(), calls=%async_computation.6 | async-start | bytes 40960 | tf_op jit(solution)/shard_map/reduce_scatter | solution.py:113
  110.2 0.7 copy-start.4
  191.4 129.8 %all-reduce.7.cloned.1.call-start = ((), (), s32[]{:S(2)}) async-start(), calls=%async_computation.9 | async-start | bytes 198656 | tf_op jit(solution)/shard_map/psum | solution.py:87
  286.1 70.7 %reduce-scatter.9.cloned.1.call-start = ((), (), s32[]{:S(2)}) async-start(), calls=%async_computation.7 | async-start | bytes 40960 | tf_op jit(solution)/shard_map/reduce_scatter | solution.py:113
  321.2 0.6 copy-start.6
  335.0 0.8 copy-start
  339.3 97.8 %reduce-scatter.11.cloned.1.call-start = ((), (), s32[]{:S(2)}) async-start(), calls=%async_computation.8 | async-start | bytes 40960 | tf_op jit(solution)/shard_map/reduce_scatter | solution.py:113
  339.3 0.7 copy-start.3
Sparse Core Ops, SparseCore 0:
  57.3 34.8 all-reduce.8
  110.2 17.3 reduce-scatter.4
  191.5 16.4 reduce-scatter.6
  286.2 34.8 all-reduce.6
  339.4 17.3 reduce-scatter.8
  420.7 16.4 reduce-scatter.10
